TPU v7x, 32 devices: a whole 2x2x4 slice. The times are simulated.
32 devices in a mesh: space: 2 (over x), energy: 16 (over z, y, core).
Axes of the slice: x: 2, y: 2, z: 4, core: 2. Of those that a mesh axis runs over, the one named last changes fastest.
Arguments:
- lesser_in: bfloat16 [16, 2, 2, 256, 256], P('energy', 'space'), may hold values from -6 to 6
- retarded: bfloat16 [16, 2, 2, 256, 256], P('energy', 'space'), may hold values from -0.25 to 0.25
- coupling: bfloat16 [2, 2, 256, 256], P('space'), may hold values from -0.25 to 0.25
- interaction: bfloat16 [2, 32, 65536], P('space', None, 'energy'), may hold values from -1.5 to 1.5
Outputs:
- self_energy: bfloat16 [16, 2, 2, 256, 256], P('energy', 'space')
All inputs are finite; a program needn't handle non-finite values.
Results may differ from a plain program's by a relative error of at most 0.029.
Values may be sent and summed in bfloat16 or wider, within the bound.
A program may use at most 128 MiB of HBM per device.

v0:
```python
import math
import jax
import jax.numpy as jnp
from jax import lax
from jax.sharding import PartitionSpec as P


def product(left_real, left_imag, right_real, right_imag):
    real_part = jnp.dot(left_real, right_real, preferred_element_type=jnp.float32) - jnp.dot(
        left_imag, right_imag, preferred_element_type=jnp.float32
    )
    imag_part = jnp.dot(left_real, right_imag, preferred_element_type=jnp.float32) + jnp.dot(
        left_imag, right_real, preferred_element_type=jnp.float32
    )
    return (real_part, imag_part)


def phase_table(row_count, column_count, length):
    row_index = jnp.arange(row_count, dtype=jnp.int32)[:, None]
    column_index = jnp.arange(column_count, dtype=jnp.int32)[None, :]
    residue = row_index * column_index % length
    return residue.astype(jnp.float32) * (2.0 * math.pi / length)


def finish(spectrum_real, spectrum_imag, weights, energy_count, length):
    forward_scale = energy_count ** (-0.5)
    inverse_scale = length ** (-0.5)
    spectrum_real = spectrum_real * forward_scale
    spectrum_imag = spectrum_imag * forward_scale
    weight_values = weights.astype(jnp.float32)
    squared_real = (
        (spectrum_real * spectrum_real - spectrum_imag * spectrum_imag) * weight_values
    ).astype(jnp.bfloat16)
    squared_imag = (2.0 * spectrum_real * spectrum_imag * weight_values).astype(jnp.bfloat16)
    inverse_phase = phase_table(energy_count, length, length)
    inverse_real = jnp.cos(inverse_phase).astype(jnp.bfloat16)
    inverse_imag = jnp.sin(inverse_phase).astype(jnp.bfloat16)
    out_real, out_imag = product(inverse_real, inverse_imag, squared_real, squared_imag)
    return jnp.stack([out_real * inverse_scale, out_imag * inverse_scale], axis=1).astype(
        jnp.bfloat16
    )


def batched(pattern, former, latter):
    return jnp.einsum(pattern, former, latter, preferred_element_type=jnp.float32)


def local(lesser_in, retarded, coupling, interaction):
    local_count = lesser_in.shape[0]
    block_order = coupling.shape[-1]
    groups = lax.axis_size("energy")
    sections = lax.axis_size("space")
    energy_count = local_count * groups
    length = 2 * energy_count
    entry_width = block_order * block_order // groups
    resolvent_real = retarded[:, 0, 0]
    resolvent_imag = retarded[:, 0, 1]
    lesser_real = lesser_in[:, 0, 0]
    lesser_imag = lesser_in[:, 0, 1]
    coupling_real = coupling[0, 0]
    coupling_imag = coupling[0, 1]
    map_real = (
        batched("eij,jk->eik", resolvent_real, coupling_real)
        - batched("eij,jk->eik", resolvent_imag, coupling_imag)
    ).astype(jnp.bfloat16)
    map_imag = (
        batched("eij,jk->eik", resolvent_real, coupling_imag)
        + batched("eij,jk->eik", resolvent_imag, coupling_real)
    ).astype(jnp.bfloat16)
    half_real = (
        batched("eij,ejk->eik", resolvent_real, lesser_real)
        - batched("eij,ejk->eik", resolvent_imag, lesser_imag)
    ).astype(jnp.bfloat16)
    half_imag = (
        batched("eij,ejk->eik", resolvent_real, lesser_imag)
        + batched("eij,ejk->eik", resolvent_imag, lesser_real)
    ).astype(jnp.bfloat16)
    source_real = batched("eij,ekj->eik", half_real, resolvent_real) + batched(
        "eij,ekj->eik", half_imag, resolvent_imag
    )
    source_imag = batched("eij,ekj->eik", half_imag, resolvent_real) - batched(
        "eij,ekj->eik", half_real, resolvent_imag
    )
    forward_phase = phase_table(length, energy_count, length)
    forward_real = jnp.cos(forward_phase).astype(jnp.bfloat16)
    forward_imag = (-jnp.sin(forward_phase)).astype(jnp.bfloat16)
    padded = (local_count + sections - 1) // sections * sections
    extra = padded - local_count
    maps_all = jnp.pad(
        jnp.stack([map_real, map_imag], axis=1), ((0, extra), (0, 0), (0, 0), (0, 0))
    )
    sources_all = jnp.pad(
        jnp.stack([source_real, source_imag], axis=1), ((0, extra), (0, 0), (0, 0), (0, 0))
    )
    maps_here, sources_here = (
        lax.all_to_all(
            maps_all[:, None].astype(jnp.float32), "space", split_axis=0, concat_axis=1, tiled=True
        ).astype(jnp.bfloat16),
        lax.all_to_all(sources_all[:, None], "space", split_axis=0, concat_axis=1, tiled=True),
    )
    per_device = maps_here.shape[0]

    def link(carried, inputs_pair):
        step_map, step_source = inputs_pair
        carry_real = (
            batched("eij,ejk->eik", step_map[:, 0], carried[:, 0])
            - batched("eij,ejk->eik", step_map[:, 1], carried[:, 1])
        ).astype(jnp.bfloat16)
        carry_imag = (
            batched("eij,ejk->eik", step_map[:, 0], carried[:, 1])
            + batched("eij,ejk->eik", step_map[:, 1], carried[:, 0])
        ).astype(jnp.bfloat16)
        grown_real = batched("eij,ekj->eik", carry_real, step_map[:, 0]) + batched(
            "eij,ekj->eik", carry_imag, step_map[:, 1]
        )
        grown_imag = batched("eij,ekj->eik", carry_imag, step_map[:, 0]) - batched(
            "eij,ekj->eik", carry_real, step_map[:, 1]
        )
        fresh = jnp.stack(
            [step_source[:, 0] + grown_real, step_source[:, 1] + grown_imag], axis=1
        ).astype(jnp.bfloat16)
        return (fresh, fresh)

    start_block = jnp.zeros((per_device, 2, block_order, block_order), jnp.bfloat16)
    last_block, layers = lax.scan(
        link, start_block, (jnp.moveaxis(maps_here, 1, 0), jnp.moveaxis(sources_here, 1, 0))
    )
    greens = jnp.moveaxis(layers, 0, 1).reshape(per_device, sections, 2, block_order * block_order)
    homed = lax.all_to_all(
        lax.all_to_all(greens, "space", split_axis=1, concat_axis=0, tiled=True),
        "energy",
        split_axis=3,
        concat_axis=0,
        tiled=True,
    )
    entries = homed.reshape(groups, padded, 2, entry_width)[:, :local_count].reshape(
        energy_count, 2, entry_width
    )
    spectrum_real, spectrum_imag = product(forward_real, forward_imag, entries[:, 0], entries[:, 1])
    result = finish(spectrum_real, spectrum_imag, interaction[0], energy_count, length)
    returned = lax.all_to_all(result, "energy", split_axis=0, concat_axis=2, tiled=True)
    return returned.reshape(local_count, 1, 2, block_order, block_order)


def solution(mesh):
    in_specs = (
        P("energy", "space", None, None, None),
        P("energy", "space", None, None, None),
        P("space", None, None, None),
        P("space", None, "energy"),
    )
    out_specs = P("energy", "space", None, None, None)
    return jax.shard_map(local, mesh=mesh, in_specs=in_specs, out_specs=out_specs, check_vma=False)
```

profile of v0, /device:TPU:0, one launch (start us, length us, event | category | flops | bytes accessed | tf_op | source)
XLA Modules:
  0.0 321.3 jit_solution(13402352093027269052)
XLA Ops:
  0.0 1.1 fusion.41
  1.2 1.2 fusion.45
  2.3 1.2 fusion.31
  3.5 1.2 fusion.32
  5.5 4.2 %all-to-all-start.1 = ((bf16[2,1,2,256,256]{4,3,2,1,0:T(8,128)(2,1)}), bf16[2,1,2,256,256]{4,3,2,1,0:T(8,128)(2,1)S(1)}, u32[]{:S(2)}, u32[]{:S(2)}) async-start(bf16[2,1,2,256,256]{4,3,2,1,0:T(8,128)(2,1)} %fusion.40), calls=%async_computation.1 | async-start | bytes 1048576 | tf_op jit(solution)/shard_map/all_to_all | solution.py:96
  9.7 1.1 fusion.47
  10.9 1.2 fusion.57
  12.0 1.2 fusion.28
  13.2 1.1 fusion.61
  14.3 1.2 fusion.27
  15.5 1.1 fusion.64
  16.6 1.1 fusion.25
  17.7 1.1 fusion.26
  18.9 1.0 fusion.33
  19.9 3.6 %all-to-all-start = ((f32[2,1,2,256,256]{4,3,2,1,0:T(8,128)}), f32[2,1,2,256,256]{4,3,2,1,0:T(8,128)S(1)}, u32[]{:S(2)}, u32[]{:S(2)}) async-start(f32[2,1,2,256,256]{4,3,2,1,0:T(8,128)} %fusion.33), calls=%async_computation | async-start | bytes 2097152 | tf_op jit(solution)/shard_map/all_to_all | solution.py:99
  23.5 14.3 %all-to-all-done = f32[2,1,2,256,256]{4,3,2,1,0:T(8,128)S(1)} async-done(((f32[2,1,2,256,256]{4,3,2,1,0:T(8,128)}), f32[2,1,2,256,256]{4,3,2,1,0:T(8,128)S(1)}, u32[]{:S(2)}, u32[]{:S(2)}) %all-to-all-start) | async-done | bytes 1048608 | tf_op jit(solution)/shard_map/all_to_all | solution.py:99
  37.9 3.7 %while.12 = (s32[]{:T(128)}, bf16[1,2,256,256]{3,2,1,0:T(8,128)(2,1)S(1)}, bf16[2,1,2,256,256]{4,3,2,1,0:T(8,128)(2,1)S(1)}, f32[2,1,2,256,256]{4,3,2,1,0:T(8,12...) while((s32[]{:T(128)}, bf16[1,2,256,256]{3,2,1,0:T(8,128)(2,1)S(1)}, ...), condition=%wide.region_1.2_spmd, body=%wide.region_0.1_spmd.sunk | while | flops 269746176 | bytes 7864409 | solution.py:125
  41.7 10.1 %all_to_all.60 = bf16[1,2,2,65536]{3,2,0,1:T(2,128)(2,1)S(1)} all-to-all(bf16[1,2,2,65536]{3,2,0,1:T(2,128)(2,1)S(1)} %reshape_transpose.3), channel_id=1, replica_groups=mesh['space'=2,'energy'=16] {'space'}, dimensions={1} | all-to-all | bytes 1048576 | tf_op jit(solution)/shard_map/all_to_all | solution.py:130
  51.8 50.9 %copy.13 = bf16[2,1,2,65536]{2,0,1,3:T(2,128)(2,1)} copy(bf16[2,1,2,65536]{3,2,0,1:T(2,128)(2,1)S(1)} %bitcast.204) | data formatting | bytes 1048576 | tf_op jit(solution)/shard_map/all_to_all | solution.py:130
  102.7 61.2 %reshape.243 = bf16[16,2,8192]{2,1,0:T(2,128)(2,1)S(1)} reshape(bf16[65536,1,2,2]{3,2,1,0:T(2,128)(2,1)} %bitcast.198) | data formatting | bytes 1048576
  163.9 20.0 %all_to_all.61 = bf16[16,2,8192]{2,1,0:T(2,128)(2,1)S(1)} all-to-all(bf16[16,2,8192]{2,1,0:T(2,128)(2,1)S(1)} %reshape.243), channel_id=1, replica_groups=mesh['space'=2,'energy'=16] {'energy'}, dimensions={0} | all-to-all | bytes 1048576 | tf_op jit(solution)/shard_map/all_to_all | solution.py:129
  183.8 73.4 %reshape.244 = bf16[65536,1,2,2]{3,2,1,0:T(2,128)(2,1)} reshape(bf16[16,2,8192]{2,1,0:T(2,128)(2,1)S(1)} %all_to_all.61) | data formatting | bytes 1048576
  257.2 46.6 %copy.17 = bf16[2,1,2,16,4096]{4,3,2,0,1:T(8,128)(2,1)S(1)} copy(bf16[2,1,2,16,4096]{2,0,4,3,1:T(2,128)(2,1)} %bitcast.199) | data formatting | bytes 1048576 | tf_op jit(solution)/shard_map/all_to_all | solution.py:129
  306.3 14.0 %all_to_all.62 = bf16[16,2,4096]{2,1,0:T(2,128)(2,1)S(1)} all-to-all(bf16[16,2,4096]{2,1,0:T(2,128)(2,1)S(1)} %copy.15), channel_id=1, replica_groups=mesh['space'=2,'energy'=16] {'energy'}, dimensions={0} | all-to-all | bytes 524288 | tf_op jit(solution)/shard_map/all_to_all | solution.py:141
  (44 shorter events, 7.9 us)
Async XLA Ops:
  5.5 14.4 %all-to-all-start.1 = ((bf16[2,1,2,256,256]{4,3,2,1,0:T(8,128)(2,1)}), bf16[2,1,2,256,256]{4,3,2,1,0:T(8,128)(2,1)S(1)}, u32[]{:S(2)}, u32[]{:S(2)}) async-start(bf16[2,1,2,256,256]{4,3,2,1,0:T(8,128)(2,1)} %fusion.40), calls=%async_computation.1 | async-start | bytes 1048576 | tf_op jit(solution)/shard_map/all_to_all | solution.py:96
  19.9 17.9 %all-to-all-start = ((f32[2,1,2,256,256]{4,3,2,1,0:T(8,128)}), f32[2,1,2,256,256]{4,3,2,1,0:T(8,128)S(1)}, u32[]{:S(2)}, u32[]{:S(2)}) async-start(f32[2,1,2,256,256]{4,3,2,1,0:T(8,128)} %fusion.33), calls=%async_computation | async-start | bytes 2097152 | tf_op jit(solution)/shard_map/all_to_all | solution.py:99
  183.8 120.8 %copy-start = (bf16[1,32,4096]{2,1,0:T(8,128)(2,1)S(1)}, bf16[1,32,4096]{2,1,0:T(8,128)(2,1)}, u32[]{:S(2)}) copy-start(bf16[1,32,4096]{2,1,0:T(8,128)(2,1)} %param.9) | copy-start | bytes 786436
where the time goes:
time: 323 us; the launch traced here: 321 us
  local copies, waits for them, and re-layouts  234 us (72%)
  blocking collectives  44 us (14%)
  matrix products  19.1 us (6%)
  waiting for transfers between devices  14.3 us (4%)
  starting transfers between devices  7.81 us (2%)
    unnamed x4, local copies, waits for them, and re-layouts  135 us
    all_to_all x1, local copies, waits for them, and re-layouts, local(): lax.all_to_all(greens, 'space', split_axis=1, concat_axis=0, tiled=True)  50.9 us
    all_to_all x1, local copies, waits for them, and re-layouts, local(): lax.all_to_all(lax.all_to_all(greens, 'space', split_axis=1, concat_axis=...  46.6 us
    all_to_all x1, blocking collectives, local(): lax.all_to_all(lax.all_to_all(greens, 'space', split_axis=1, concat_axis=...  20 us
    dot_general x28, matrix products, batched(): jnp.einsum(pattern, former, latter, preferred_element_type=jnp.float32)  17 us
    all_to_all x1, waiting for transfers between devices, local(): lax.all_to_all(sources_all[:, None], 'space', split_axis=0, concat_axis=1...  14.3 us
    all_to_all x1, blocking collectives, local(): lax.all_to_all(result, 'energy', split_axis=0, concat_axis=2, tiled=True)  14 us
    all_to_all x1, blocking collectives, local(): lax.all_to_all(greens, 'space', split_axis=1, concat_axis=0, tiled=True)  10.1 us
  transfers between devices with their start and end apart: 2, of which 1 were waited for; matrix products, arithmetic and copies ran while one was open for 3% of the time, Pallas kernels for 0%

commit v1 on v0

--- a/solution.py
+++ b/solution.py
@@ -126,12 +126,20 @@
         link, start_block, (jnp.moveaxis(maps_here, 1, 0), jnp.moveaxis(sources_here, 1, 0))
     )
     greens = jnp.moveaxis(layers, 0, 1).reshape(per_device, sections, 2, block_order * block_order)
-    homed = lax.all_to_all(
-        lax.all_to_all(greens, "space", split_axis=1, concat_axis=0, tiled=True),
-        "energy",
-        split_axis=3,
-        concat_axis=0,
-        tiled=True,
+    homed = jnp.concatenate(
+        lax.all_to_all(
+            jnp.stack(
+                jnp.split(
+                    lax.all_to_all(greens, "space", split_axis=1, concat_axis=0, tiled=True),
+                    lax.axis_size("energy"),
+                    axis=3,
+                )
+            ),
+            "energy",
+            0,
+            0,
+        ),
+        axis=0,
     )
     entries = homed.reshape(groups, padded, 2, entry_width)[:, :local_count].reshape(
         energy_count, 2, entry_width

time: 323 us -> 85.6 us (0.27)
  local copies, waits for them, and re-layouts: 234 us -> 3.51 us
  matrix products: 19.1 us -> 8.97 us
  waiting for transfers between devices: 14.3 us -> 19.3 us
    unnamed x4 -> x23, local copies, waits for them, and re-layouts: 135 us -> 1.14 us
    all_to_all x2 -> x0, local copies, waits for them, and re-layouts: 97.4 us -> none  [the longest x1 50.9 us: local(): lax.all_to_all(greens, 'space', split_axis=1, concat_axis=0, tiled=True)]
    dot_general x28, matrix products: 17 us -> 6.64 us  [batched(): jnp.einsum(pattern, former, latter, preferred_element_type=jnp.float32)]
    all_to_all x1, waiting for transfers between devices: 0.01 us -> 6 us  [local(): lax.all_to_all(maps_all[:, None].astype(jnp.float32), 'space', split_axis...]
  transfers between devices with their start and end apart: 2 -> 2, of which waited for: 1 -> 2; matrix products, arithmetic and copies ran while one was open for 3% -> 3% of each run, Pallas kernels for 0% -> 0%
where the time goes in v1:
time: 85.6 us; the launch traced here: 85.1 us
  blocking collectives  43 us (50%)
  waiting for transfers between devices  19.3 us (23%)
  matrix products  8.97 us (10%)
  starting transfers between devices  7.94 us (9%)
  local copies, waits for them, and re-layouts  3.51 us (4%)
  other arithmetic  2.05 us (2%)
    all_to_all x1, blocking collectives, local(): lax.all_to_all(jnp.stack(jnp.split(lax.all_to_all(greens, 'space', split_...  19.7 us
    all_to_all x1, blocking collectives, local(): lax.all_to_all(result, 'energy', split_axis=0, concat_axis=2, tiled=True)  14 us
    all_to_all x1, waiting for transfers between devices, local(): lax.all_to_all(sources_all[:, None], 'space', split_axis=0, concat_axis=1...  13.3 us
    all_to_all x1, blocking collectives, local(): lax.all_to_all(greens, 'space', split_axis=1, concat_axis=0, tiled=True)  9.24 us
    dot_general x28, matrix products, batched(): jnp.einsum(pattern, former, latter, preferred_element_type=jnp.float32)  6.64 us
    all_to_all x1, waiting for transfers between devices, local(): lax.all_to_all(maps_all[:, None].astype(jnp.float32), 'space', split_axis...  6 us
    all_to_all x1, starting transfers between devices, local(): lax.all_to_all(maps_all[:, None].astype(jnp.float32), 'space', split_axis...  4.36 us
    all_to_all x1, starting transfers between devices, local(): lax.all_to_all(sources_all[:, None], 'space', split_axis=0, concat_axis=1...  3.58 us
  transfers between devices with their start and end apart: 2, of which 2 were waited for; matrix products, arithmetic and copies ran while one was open for 3% of the time, Pallas kernels for 0%

profile of v1, /device:TPU:0, one launch (start us, length us, event | category | flops | bytes accessed | tf_op | source)
XLA Modules:
  0.0 85.1 jit_solution(2266567847947035270)
XLA Ops:
  0.0 1.2 %fusion.47 = f32[256,256]{1,0:T(8,128)S(1)} fusion(bf16[1,2,256,256]{3,2,1,0:T(8,128)(2,1)} %param.8, bf16[1,1,2,256,256]{4,3,2,1,0:T(8,128)(2,1)} %param.7), kind=kOutput, calls=%fused_computation.75 | convolution fusion | flops 33554432 | bytes 524288 | tf_op jit(solution)/shard_map/eij,jk->eik/dot_general | solution.py:45
  1.8 0.9 %fusion.40 = bf16[2,1,2,256,256]{4,3,2,1,0:T(8,128)(2,1)} fusion(bf16[1,1,256,256]{3,2,1,0:T(8,128)(2,1)S(1)} %fusion.31, bf16[1,1,256,256]{3,2,1,0:T(8,128)(2,1)S(1)} %fusion.32), kind=kLoop, calls=%fused_computation.66 | loop fusion | flops 1835008 | bytes 786432 | tf_op jit(solution)/shard_map/convert_element_type | solution.py:97
  2.7 4.4 %all-to-all-start.1 = ((bf16[2,1,2,256,256]{4,3,2,1,0:T(8,128)(2,1)}), bf16[2,1,2,256,256]{4,3,2,1,0:T(8,128)(2,1)S(1)}, u32[]{:S(2)}, u32[]{:S(2)}) async-start(bf16[2,1,2,256,256]{4,3,2,1,0:T(8,128)(2,1)} %fusion.40), calls=%async_computation.1 | async-start | bytes 1048576 | tf_op jit(solution)/shard_map/all_to_all | solution.py:96
  8.3 0.2 fusion.25
  8.5 0.2 fusion.26
  8.7 1.0 %fusion.33 = f32[2,1,2,256,256]{4,3,2,1,0:T(8,128)} fusion(f32[1,1,256,256]{3,2,1,0:T(8,128)S(1)} %fusion.25, f32[1,1,256,256]{3,2,1,0:T(8,128)S(1)} %fusion.26), kind=kLoop, calls=%fused_computation.56 | loop fusion | flops 1048576 | bytes 1572864 | tf_op jit(solution)/shard_map/broadcast_in_dim | solution.py:99
  9.8 6.0 %all-to-all-done.1 = bf16[2,1,2,256,256]{4,3,2,1,0:T(8,128)(2,1)S(1)} async-done(((bf16[2,1,2,256,256]{4,3,2,1,0:T(8,128)(2,1)}), bf16[2,1,2,256,256]{4,3,2,1,0:T(8,128)(2,1)S(1)}, u32[]{:S(2)}, u32[]{:S(2)}) %all-to-all-start.1) | async-done | bytes 524320 | tf_op jit(solution)/shard_map/all_to_all | solution.py:96
  15.8 3.6 %all-to-all-start = ((f32[2,1,2,256,256]{4,3,2,1,0:T(8,128)}), f32[2,1,2,256,256]{4,3,2,1,0:T(8,128)S(1)}, u32[]{:S(2)}, u32[]{:S(2)}) async-start(f32[2,1,2,256,256]{4,3,2,1,0:T(8,128)} %fusion.33), calls=%async_computation | async-start | bytes 2097152 | tf_op jit(solution)/shard_map/all_to_all | solution.py:99
  19.4 13.3 %all-to-all-done = f32[2,1,2,256,256]{4,3,2,1,0:T(8,128)S(1)} async-done(((f32[2,1,2,256,256]{4,3,2,1,0:T(8,128)}), f32[2,1,2,256,256]{4,3,2,1,0:T(8,128)S(1)}, u32[]{:S(2)}, u32[]{:S(2)}) %all-to-all-start) | async-done | bytes 1048608 | tf_op jit(solution)/shard_map/all_to_all | solution.py:99
  32.7 3.7 %while.12 = (s32[]{:T(128)}, bf16[1,2,256,256]{3,2,1,0:T(8,128)(2,1)S(1)}, bf16[2,1,2,256,256]{4,3,2,1,0:T(8,128)(2,1)S(1)}, f32[2,1,2,256,256]{4,3,2,1,0:T(8,12...) while((s32[]{:T(128)}, bf16[1,2,256,256]{3,2,1,0:T(8,128)(2,1)S(1)}, ...), condition=%wide.region_1.2_spmd, body=%wide.region_0.1_spmd.sunk | while | flops 269746176 | bytes 7864401 | solution.py:125
  33.8 0.2 fusion.187
  35.6 0.2 fusion.187
  36.1 0.2 fusion.185
  36.6 9.2 %all_to_all.50 = bf16[1,2,2,65536]{3,2,0,1:T(2,128)(2,1)S(1)} all-to-all(bf16[1,2,2,65536]{3,2,0,1:T(2,128)(2,1)S(1)} %reshape_transpose.3), channel_id=1, replica_groups=mesh['space'=2,'energy'=16] {'space'}, dimensions={1} | all-to-all | bytes 1048576 | tf_op jit(solution)/shard_map/all_to_all | solution.py:133
  46.4 19.7 %all_to_all.51 = bf16[16,2,1,2,4096]{4,3,1,2,0:T(2,128)(2,1)S(1)} all-to-all(bf16[16,2,1,2,4096]{4,3,1,2,0:T(2,128)(2,1)S(1)} %constant_dynamic-update-slice_fusion), channel_id=1, replica_groups=mesh['space'=2,'energy'=16] {'energy'}, dimensions={0} | all-to-all | bytes 1048576 | tf_op jit(solution)/shard_map/all_to_all | solution.py:130
  66.3 0.6 fusion.143
  66.9 0.3 fusion.45
  67.2 0.3 fusion.41
  67.6 0.3 convolution_subtract_fusion.2
  67.9 0.6 copy-done.3
  68.5 0.4 fusion.36
  69.9 0.3 copy.31
  70.2 14.0 %all_to_all.52 = bf16[16,2,4096]{2,1,0:T(2,128)(2,1)S(1)} all-to-all(bf16[16,2,4096]{2,1,0:T(2,128)(2,1)S(1)} %copy.31), channel_id=1, replica_groups=mesh['space'=2,'energy'=16] {'energy'}, dimensions={0} | all-to-all | bytes 524288 | tf_op jit(solution)/shard_map/all_to_all | solution.py:149
  84.3 0.8 reshape.235
  (63 shorter events, 6.6 us)
Async XLA Ops:
  0.0 1.2 %copy-start = (bf16[1,1,2,256,256]{4,3,2,1,0:T(8,128)(2,1)S(1)}, bf16[1,1,2,256,256]{4,3,2,1,0:T(8,128)(2,1)}, u32[]{:S(2)}) copy-start(bf16[1,1,2,256,256]{4,3,2,1,0:T(8,128)(2,1)} %param.7) | copy-start | bytes 786436
  0.0 1.2 %copy-start.1 = (bf16[1,2,256,256]{3,2,1,0:T(8,128)(2,1)S(1)}, bf16[1,2,256,256]{3,2,1,0:T(8,128)(2,1)}, u32[]{:S(2)}) copy-start(bf16[1,2,256,256]{3,2,1,0:T(8,128)(2,1)} %param.8) | copy-start | bytes 786436
  2.7 4.4 %copy-start.2 = (bf16[1,1,2,256,256]{4,3,2,1,0:T(8,128)(2,1)S(1)}, bf16[1,1,2,256,256]{4,3,2,1,0:T(8,128)(2,1)}, u32[]{:S(2)}) copy-start(bf16[1,1,2,256,256]{4,3,2,1,0:T(8,128)(2,1)} %param.6) | copy-start | bytes 786436
  2.7 13.1 %all-to-all-start.1 = ((bf16[2,1,2,256,256]{4,3,2,1,0:T(8,128)(2,1)}), bf16[2,1,2,256,256]{4,3,2,1,0:T(8,128)(2,1)S(1)}, u32[]{:S(2)}, u32[]{:S(2)}) async-start(bf16[2,1,2,256,256]{4,3,2,1,0:T(8,128)(2,1)} %fusion.40), calls=%async_computation.1 | async-start | bytes 1048576 | tf_op jit(solution)/shard_map/all_to_all | solution.py:96
  15.8 16.9 %all-to-all-start = ((f32[2,1,2,256,256]{4,3,2,1,0:T(8,128)}), f32[2,1,2,256,256]{4,3,2,1,0:T(8,128)S(1)}, u32[]{:S(2)}, u32[]{:S(2)}) async-start(f32[2,1,2,256,256]{4,3,2,1,0:T(8,128)} %fusion.33), calls=%async_computation | async-start | bytes 2097152 | tf_op jit(solution)/shard_map/all_to_all | solution.py:99
  67.6 1.0 %copy-start.3 = (bf16[1,32,4096]{2,1,0:T(8,128)(2,1)S(1)}, bf16[1,32,4096]{2,1,0:T(8,128)(2,1)}, u32[]{:S(2)}) copy-start(bf16[1,32,4096]{2,1,0:T(8,128)(2,1)} %param.9) | copy-start | bytes 786436
